TPU v7x, 16 devices: a whole 2x2x2 slice. The times are simulated.
16 devices in a mesh: rep: 1, r: 2 (over z), s: 8 (over x, y, core).
Axes of the slice: x: 2, y: 2, z: 2, core: 2. Of those that a mesh axis runs over, the one named last changes fastest.
Arguments:
- x: bfloat16 [16, 2048, 1280], P(('rep', 'r', 's'))
- dy: bfloat16 [16, 2048, 1280], P(('rep', 'r', 's'))
- w_gate: bfloat16 [2, 1280, 4096], P(None, 's')
- w_up: bfloat16 [2, 1280, 4096], P(None, 's')
- w_down: bfloat16 [2, 4096, 1280], P(None, 's')
Outputs:
- output 1: bfloat16 [16, 2048, 1280], P(('rep', 'r', 's'))
- output 2: bfloat16 [2, 1280, 4096], P('rep', 's')
- output 3: bfloat16 [2, 1280, 4096], P('rep', 's')
- output 4: bfloat16 [2, 4096, 1280], P('rep', 's')
All inputs are finite; a program needn't handle non-finite values.
Results may differ from a plain program's by a relative error of at most 0.018.
Values are sent between devices in bfloat16 or wider.
A program may use at most 2 GiB of HBM per device.

v0:
```python
import jax
import jax.numpy as jnp
from jax import lax
from jax.sharding import PartitionSpec as P

NAMES = ("w_gate", "w_up", "w_down")


def matmul(a, w):
    return jnp.dot(a, w, preferred_element_type=jnp.float32).astype(jnp.bfloat16)


def normed(h):
    wide = h.astype(jnp.float32)
    scale = lax.rsqrt(jnp.mean(wide**2, -1, keepdims=True) + 1e-6)
    return (wide * scale).astype(jnp.bfloat16)


def layer(h, w):
    a = normed(h)
    gate = jnp.dot(a, w["w_gate"], preferred_element_type=jnp.float32)
    up = jnp.dot(a, w["w_up"], preferred_element_type=jnp.float32)
    return h + matmul((jax.nn.silu(gate) * up).astype(jnp.bfloat16), w["w_down"])


def solution(mesh):
    def fetched(weights, number):
        return {name: lax.all_gather(w[number], "s", axis=0, tiled=True) for name, w in zip(NAMES, weights, strict=True)}

    def summed(term):
        return lax.psum(lax.psum_scatter(term, "s", scatter_dimension=0, tiled=True), "r")

    def step(x, dy, *weights):
        layers = weights[0].shape[0]
        h, inputs = x[0], []
        for number in range(layers):
            inputs.append(h)
            h = layer(h, fetched(weights, number))
        by_h, mine = dy[0], [None] * layers
        for number in reversed(range(layers)):
            _, back = jax.vjp(lambda w, h: layer(h, w), fetched(weights, number), inputs[number])
            by_w, by_h = back(by_h)
            mine[number] = [summed(by_w[name]) for name in NAMES]
        return (by_h[None], *(jnp.stack([mine[number][i] for number in range(layers)]) for i in range(3)))

    states, cut = P(("rep", "r", "s"), None, None), P(None, "s", None)
    return jax.shard_map(
        step,
        mesh=mesh,
        in_specs=(states, states) + (cut,) * 3,
        out_specs=(states,) + (P("rep", "s", None),) * 3,
        check_vma=False,
    )
```

profile of v0, /device:TPU:0, one launch (start us, length us, event | category | flops | bytes accessed | tf_op | source)
XLA Modules:
  0.0 1161.9 jit_solution(2206152538160754101)
XLA Ops:
  7.2 0.0 all-gather.13.cloned.1.call-start
  7.2 3.6 fusion.88
  10.9 0.0 all-gather.13.cloned.1.call-update
  10.9 0.0 all-gather.15.cloned.1.call-start
  10.9 3.5 fusion.87
  14.5 0.0 all-gather.15.cloned.1.call-update
  14.5 0.0 all-gather.17.cloned.1.call-start
  14.5 1.7 fusion.86
  16.2 0.0 all-gather.17.cloned.1.call-update
  16.2 0.0 all-gather.21.cloned.1.call-start
  16.3 0.5 all-gather.21.cloned.1.call-update
  16.8 0.0 all-gather.23.cloned.1.call-start
  16.9 0.5 all-gather.23.cloned.1.call-update
  17.4 0.0 all-gather.19.cloned.1.call-start
  17.4 0.5 all-gather.19.cloned.1.call-update
  18.0 0.0 reduce-scatter.17.cloned.1.call-start
  18.0 7.9 copy.10
  25.9 3.6 fusion.18
  29.5 0.6 copy-done.1
  30.1 7.9 copy.9
  38.0 35.1 %all-gather.13.cloned.1.call-done = bf16[1,1280,4096]{2,1,0:T(8,128)(2,1)} async-done(((bf16[1,160,4096]{2,1,0:T(8,128)(2,1)}), bf16[1,1280,4096]{2,1,0:T(8,128)(2,1)}) %all-gather.13.cloned.1.call-update) | async-done | bytes 10485776 | tf_op jit(solution)/shard_map/all_gather | solution.py:28
  73.1 29.4 %fusion.40 = f32[2048,4096]{1,0:T(8,128)} fusion(bf16[1,1280,4096]{2,1,0:T(8,128)(2,1)} %all-gather.13.cloned.1.call-done, bf16[1,2048,1280]{1,2,0:T(8,128)(2,1)} %copy.10, f32[2048]{0:T(1024)S(1)} %fusion.79), kind=kOutput, calls=%fused_computation.65 | convolution fusion | flops 21482700800 | bytes 49291264 | tf_op jit(solution)/shard_map/dot_general | solution.py:21
  102.5 31.7 %all-gather.15.cloned.1.call-done = bf16[1,1280,4096]{2,1,0:T(8,128)(2,1)} async-done(((bf16[1,160,4096]{2,1,0:T(8,128)(2,1)}), bf16[1,1280,4096]{2,1,0:T(8,128)(2,1)}) %all-gather.15.cloned.1.call-update) | async-done | bytes 10485776 | tf_op jit(solution)/shard_map/all_gather | solution.py:28
  134.2 41.8 %multiply_convert_fusion.1 = (bf16[2048,4096]{1,0:T(8,128)(2,1)}, f32[2048,4096]{1,0:T(8,128)}) fusion(f32[2048,4096]{1,0:T(8,128)} %fusion.40, bf16[1,1280,4096]{2,1,0:T(8,128)(2,1)} %all-gather.15.cloned.1.call-done, bf16[1,2048,1280]{1,2,0:T(8,128)(2,1)} %copy.10, f32[2048]{0:T(1024)S(1)} %fusion.79), kind=kOutput, calls=%fused_computation.13 | convolution fusion | flops 21533032448 | bytes 99622912 | tf_op jit(solution)/shard_map/dot_general | solution.py:22
  176.0 19.3 %all-gather.17.cloned.1.call-done = bf16[1,4096,1280]{2,1,0:T(8,128)(2,1)} async-done(((bf16[1,512,1280]{2,1,0:T(8,128)(2,1)}), bf16[1,4096,1280]{2,1,0:T(8,128)(2,1)}) %all-gather.17.cloned.1.call-update) | async-done | bytes 10485776 | tf_op jit(solution)/shard_map/all_gather | solution.py:28
  195.3 30.3 %fusion.21 = (f32[2048]{0:T(1024)S(1)}, bf16[2048,1280]{0,1:T(8,128)(2,1)}) fusion(bf16[2048,4096]{1,0:T(8,128)(2,1)} %get-tuple-element.20, bf16[1,4096,1280]{2,1,0:T(8,128)(2,1)} %all-gather.17.cloned.1.call-done, bf16[1,2048,1280]{1,2,0:T(8,128)(2,1)} %copy.10), kind=kOutput, calls=%fused_computation.46 | convolution fusion | flops 21487941632 | bytes 37756928 | tf_op jit(solution)/shard_map/dot_general | solution.py:10
  225.6 30.6 %all-gather.21.cloned.1.call-done = bf16[1,4096,1280]{2,1,0:T(8,128)(2,1)} async-done(((bf16[1,512,1280]{2,1,0:T(8,128)(2,1)}), bf16[1,4096,1280]{2,1,0:T(8,128)(2,1)}) %all-gather.21.cloned.1.call-update) | async-done | bytes 10485776 | tf_op jit(solution)/shard_map/all_gather | solution.py:28
  256.2 28.9 %convolution_convert_fusion.4 = bf16[2048,4096]{1,0:T(8,128)(2,1)} fusion(bf16[1,4096,1280]{2,1,0:T(8,128)(2,1)} %all-gather.21.cloned.1.call-done, bf16[1,2048,1280]{2,1,0:T(8,128)(2,1)} %param.6), kind=kOutput, calls=%fused_computation.36 | convolution fusion | flops 21483225088 | bytes 32505856 | tf_op jit(solution)/shard_map/transpose(jvp())/dot_general | solution.py:10
  285.1 32.7 %all-gather.23.cloned.1.call-done = bf16[1,1280,4096]{2,1,0:T(8,128)(2,1)} async-done(((bf16[1,160,4096]{2,1,0:T(8,128)(2,1)}), bf16[1,1280,4096]{2,1,0:T(8,128)(2,1)}) %all-gather.23.cloned.1.call-update) | async-done | bytes 10485776 | tf_op jit(solution)/shard_map/all_gather | solution.py:28
  317.7 29.5 %fusion.24 = f32[2048,4096]{1,0:T(8,128)} fusion(bf16[1,1280,4096]{2,1,0:T(8,128)(2,1)} %all-gather.23.cloned.1.call-done, bf16[2048,1280]{0,1:T(8,128)(2,1)} %get-tuple-element.23, f32[2048]{0:T(1024)S(1)} %fusion.80), kind=kOutput, calls=%fused_computation.49 | convolution fusion | flops 21482700800 | bytes 49291264 | tf_op jit(solution)/shard_map/jvp()/dot_general | solution.py:22
  347.2 32.0 %all-gather.19.cloned.1.call-done = bf16[1,1280,4096]{2,1,0:T(8,128)(2,1)} async-done(((bf16[1,160,4096]{2,1,0:T(8,128)(2,1)}), bf16[1,1280,4096]{2,1,0:T(8,128)(2,1)}) %all-gather.19.cloned.1.call-update) | async-done | bytes 10485776 | tf_op jit(solution)/shard_map/all_gather | solution.py:28
  379.2 49.9 %fusion.1 = (bf16[2048,4096]{1,0:T(8,128)(2,1)}, f32[2048,4096]{1,0:T(8,128)}) fusion(f32[2048,4096]{1,0:T(8,128)} %fusion.24, bf16[2048,4096]{1,0:T(8,128)(2,1)} %convolution_convert_fusion.4, bf16[1,1280,4096]{2,1,0:T(8,128)(2,1)} %all-gather.19.cloned.1.call-done, bf16[2048,1280]{0,1:T(8,128)(2,1)} %get-tuple-element.23, f32[2048]{0:T(1024)S(1)} %fusion.80), kind=kOutput, calls=%fused_computation.7 | convolution fusion | flops 21583364096 | bytes 116400128 | tf_op jit(solution)/shard_map/jvp()/dot_general | solution.py:21
  429.2 35.4 %fusion.11 = bf16[4096,1280]{1,0:T(8,128)(2,1)} fusion(f32[2048,4096]{1,0:T(8,128)} %fusion.24, bf16[1,2048,1280]{2,1,0:T(8,128)(2,1)} %param.6, f32[2048,4096]{1,0:T(8,128)} %get-tuple-element.25), kind=kOutput, calls=%fused_computation.31 | convolution fusion | flops 21530411008 | bytes 82837504 | tf_op jit(solution)/shard_map/transpose(jvp())/dot_general | solution.py:10
  464.6 0.0 reduce-scatter.17.cloned.1.call-update
  464.6 0.0 reduce-scatter.15.cloned.1.call-start
  464.6 29.1 %fusion.54 = bf16[2048,1280]{0,1:T(8,128)(2,1)} fusion(bf16[2048,4096]{1,0:T(8,128)(2,1)} %get-tuple-element.24, bf16[1,1280,4096]{2,1,0:T(8,128)(2,1)} %all-gather.19.cloned.1.call-done), kind=kOutput, calls=%fused_computation.71 | convolution fusion | flops 21474836480 | bytes 32505856 | tf_op jit(solution)/shard_map/transpose(jvp())/dot_general | solution.py:21
  493.7 37.1 %fusion.23 = (f32[2048]{0:T(1024)S(1)}, bf16[2048,1280]{0,1:T(8,128)(2,1)}) fusion(bf16[2048,1280]{0,1:T(8,128)(2,1)} %get-tuple-element.23, bf16[2048,1280]{0,1:T(8,128)(2,1)} %fusion.54, bf16[1,1280,4096]{2,1,0:T(8,128)(2,1)} %all-gather.23.cloned.1.call-done, bf16[2048,4096]{1,0:T(8,128)(2,1)} %convolution_convert_fusion.4, ...), kind=kOutput, calls=%fused_computation.48 | convolution fusion | flops 21540894720 | bytes 76554240 | tf_op jit(solution)/shard_map/transpose(jvp())/dot_general | solution.py:22
  530.9 12.3 %fusion.68 = bf16[2048,1280]{0,1:T(8,128)(2,1)} fusion(bf16[2048,1280]{0,1:T(8,128)(2,1)} %get-tuple-element.23, bf16[2048,1280]{0,1:T(8,128)(2,1)} %get-tuple-element.27, bf16[1,2048,1280]{1,2,0:T(8,128)(2,1)} %copy.9, f32[2048]{0:T(1024)S(1)} %multiply_multiply_fusion.1, f32[2048]{0:T(1024)S(1)} %copy-done.6), kind=kLoop, calls=%fused_computation.77 | loop fusion | flops 18350080 | bytes 20987904 | tf_op jit(solution)/shard_map/transpose(jvp())/add_any | solution.py:14
  543.1 28.0 %convolution_convert_fusion.2 = bf16[4096,1280]{1,0:T(8,128)(2,1)} fusion(bf16[2048,4096]{1,0:T(8,128)(2,1)} %get-tuple-element.20, bf16[2048,1280]{0,1:T(8,128)(2,1)} %fusion.68), kind=kOutput, calls=%fused_computation.34 | convolution fusion | flops 21480079360 | bytes 32505856 | tf_op jit(solution)/shard_map/transpose(jvp())/dot_general | solution.py:10
  571.2 0.0 reduce-scatter.15.cloned.1.call-update
  571.2 0.0 reduce-scatter.11.cloned.1.call-start
  571.3 47.6 %fusion.3 = (bf16[2048,4096]{1,0:T(8,128)(2,1)}, bf16[2048,4096]{1,0:T(8,128)(2,1)}) fusion(f32[2048,4096]{1,0:T(8,128)} %fusion.40, f32[2048,4096]{1,0:T(8,128)} %get-tuple-element.21, bf16[2048,1280]{0,1:T(8,128)(2,1)} %fusion.68, bf16[1,4096,1280]{2,1,0:T(8,128)(2,1)} %all-gather.17.cloned.1.call-done), kind=kOutput, calls=%fused_computation.9 | convolution fusion | flops 21583888384 | bytes 116391936 | tf_op jit(solution)/shard_map/transpose(jvp())/dot_general | solution.py:10
  618.9 29.5 %fusion.12 = bf16[1280,4096]{1,0:T(8,128)(2,1)} fusion(bf16[2048,4096]{1,0:T(8,128)(2,1)} %get-tuple-element.29, bf16[1,2048,1280]{1,2,0:T(8,128)(2,1)S(1)} %bitcast.93, f32[2048]{0:T(1024)S(1)} %copy-done.4, f32[2048,4096]{1,0:T(8,128)} %fusion.40), kind=kOutput, calls=%fused_computation.32 | convolution fusion | flops 21538275328 | bytes 66068480 | tf_op jit(solution)/shard_map/transpose(jvp())/dot_general | solution.py:22
  648.4 0.0 reduce-scatter.11.cloned.1.call-update
  648.5 0.0 reduce-scatter.13.cloned.1.call-start
  648.5 0.6 copy-done.7
  649.1 30.8 %fusion.13 = bf16[1280,4096]{1,0:T(8,128)(2,1)} fusion(bf16[2048,4096]{1,0:T(8,128)(2,1)} %convolution_convert_fusion.4, bf16[2048,1280]{0,1:T(8,128)(2,1)} %get-tuple-element.23, f32[2048]{0:T(1024)S(1)} %copy-done.7, f32[2048,4096]{1,0:T(8,128)} %get-tuple-element.25), kind=kOutput, calls=%fused_computation.33 | convolution fusion | flops 21538275328 | bytes 66068480 | tf_op jit(solution)/shard_map/transpose(jvp())/dot_general | solution.py:22
  680.0 0.0 reduce-scatter.13.cloned.1.call-update
  680.0 0.0 reduce-scatter.9.cloned.1.call-start
  680.0 27.8 %convolution_convert_fusion = bf16[1280,4096]{1,0:T(8,128)(2,1)} fusion(bf16[2048,4096]{1,0:T(8,128)(2,1)} %get-tuple-element.24, bf16[2048,1280]{0,1:T(8,128)(2,1)} %get-tuple-element.23, f32[2048]{0:T(1024)S(1)} %copy-done.7), kind=kOutput, calls=%fused_computation.29 | convolution fusion | flops 21482700800 | bytes 32514048 | tf_op jit(solution)/shard_map/transpose(jvp())/dot_general | solution.py:21
  707.9 0.0 reduce-scatter.7.cloned.1.call-start
  707.9 27.8 %convolution_convert_fusion.1 = bf16[1280,4096]{1,0:T(8,128)(2,1)} fusion(bf16[2048,4096]{1,0:T(8,128)(2,1)} %get-tuple-element.28, bf16[1,2048,1280]{1,2,0:T(8,128)(2,1)} %copy.10, f32[2048]{0:T(1024)S(1)} %copy-done.4), kind=kOutput, calls=%fused_computation.30 | convolution fusion | flops 21482700800 | bytes 32514048 | tf_op jit(solution)/shard_map/transpose(jvp())/dot_general | solution.py:21
  735.8 0.0 all-reduce.3.cloned.1.call-start
  735.8 29.2 %fusion.51 = bf16[2048,1280]{0,1:T(8,128)(2,1)} fusion(bf16[2048,4096]{1,0:T(8,128)(2,1)} %get-tuple-element.28, bf16[1,1280,4096]{2,1,0:T(8,128)(2,1)} %all-gather.13.cloned.1.call-done), kind=kOutput, calls=%fused_computation.70 | convolution fusion | flops 21474836480 | bytes 32505856 | tf_op jit(solution)/shard_map/transpose(jvp())/dot_general | solution.py:21
  765.0 38.7 %reduce-scatter.13.cloned.1.call-done = bf16[160,4096]{1,0:T(8,128)(2,1)} async-done(((bf16[1280,4096]{1,0:T(8,128)(2,1)}), bf16[160,4096]{1,0:T(8,128)(2,1)}) %reduce-scatter.13.cloned.1.call-update) | async-done | bytes 1310736 | tf_op jit(solution)/shard_map/reduce_scatter | solution.py:31
  803.7 78.7 %reduce-scatter.9.cloned.1.call-done = bf16[160,4096]{1,0:T(8,128)(2,1)} async-done(((bf16[1280,4096]{1,0:T(8,128)(2,1)}), bf16[160,4096]{1,0:T(8,128)(2,1)}) %reduce-scatter.9.cloned.1.call-update) | async-done | bytes 1310736 | tf_op jit(solution)/shard_map/reduce_scatter | solution.py:31
  882.4 78.5 %reduce-scatter.7.cloned.1.call-done = bf16[160,4096]{1,0:T(8,128)(2,1)} async-done(((bf16[1280,4096]{1,0:T(8,128)(2,1)}), bf16[160,4096]{1,0:T(8,128)(2,1)}) %reduce-scatter.7.cloned.1.call-update) | async-done | bytes 1310736 | tf_op jit(solution)/shard_map/reduce_scatter | solution.py:31
  960.9 0.0 all-reduce.3.cloned.1.call-update
  960.9 37.2 %fusion.20 = (f32[2048]{0:T(1024)S(1)}, bf16[2048,1280]{0,1:T(8,128)(2,1)}) fusion(bf16[1,2048,1280]{1,2,0:T(8,128)(2,1)} %copy.10, bf16[2048,1280]{0,1:T(8,128)(2,1)} %fusion.51, bf16[1,1280,4096]{2,1,0:T(8,128)(2,1)} %all-gather.15.cloned.1.call-done, bf16[2048,4096]{1,0:T(8,128)(2,1)} %get-tuple-element.29, f32[2048,4096]{1,0:T(8,128)} %fusion.40), kind=kOutput, calls=%fused_computation.45 | convolution fusion | flops 21540894720 | bytes 76554240 | tf_op jit(solution)/shard_map/transpose(jvp())/dot_general | solution.py:22
  998.1 12.3 %fusion.67 = bf16[1,2048,1280]{1,2,0:T(8,128)(2,1)} fusion(bf16[2048,1280]{0,1:T(8,128)(2,1)} %fusion.68, bf16[2048,1280]{0,1:T(8,128)(2,1)} %get-tuple-element.31, bf16[1,2048,1280]{1,2,0:T(8,128)(2,1)} %copy.10, f32[2048]{0:T(1024)S(1)} %multiply_multiply_fusion, f32[2048]{0:T(1024)S(1)} %copy-done.4), kind=kLoop, calls=%fused_computation.76 | loop fusion | flops 18350080 | bytes 20987904 | tf_op jit(solution)/shard_map/broadcast_in_dim | solution.py:44
  1010.4 7.9 copy.11
  1018.2 129.0 %all-reduce.3.cloned.1.call-done = (bf16[1,160,4096]{2,1,0:T(8,128)(2,1)}, bf16[1,160,4096]{2,1,0:T(8,128)(2,1)}, bf16[1,160,4096]{2,1,0:T(8,128)(2,1)}, bf16[1,...) async-done(((bf16[1,160,4096]{2,1,0:T(8,128)(2,1)}, bf16[1,160,4096]{2,1,0:T(8,128)(2,1)}, bf16[1,160,4096]{2,1,0:T(8,128)(2,1)}, ...) | async-done | bytes 7864336 | tf_op jit(solution)/shard_map/psum | solution.py:31
  1147.2 3.4 pad_maximum_fusion.2
  1150.7 4.3 pad_maximum_fusion
  (32 shorter events, 0.1 us)
Async XLA Ops:
  7.2 7.4 copy-start
  7.2 65.9 %all-gather.13.cloned.1.call-start = ((), (), s32[]{:S(2)}) async-start(), calls=%async_computation.12 | async-start | bytes 11796480 | tf_op jit(solution)/shard_map/all_gather | solution.py:28
  10.9 123.3 %all-gather.15.cloned.1.call-start = ((), (), s32[]{:S(2)}) async-start(), calls=%async_computation.13 | async-start | bytes 11796480 | tf_op jit(solution)/shard_map/all_gather | solution.py:28
  14.5 180.8 %all-gather.17.cloned.1.call-start = ((), (), s32[]{:S(2)}) async-start(), calls=%async_computation.14 | async-start | bytes 11796480 | tf_op jit(solution)/shard_map/all_gather | solution.py:28
  16.2 240.0 %all-gather.21.cloned.1.call-start = ((), (), s32[]{:S(2)}) async-start(), calls=%async_computation.16 | async-start | bytes 11796480 | tf_op jit(solution)/shard_map/all_gather | solution.py:28
  16.8 300.9 %all-gather.23.cloned.1.call-start = ((), (), s32[]{:S(2)}) async-start(), calls=%async_computation.17 | async-start | bytes 11796480 | tf_op jit(solution)/shard_map/all_gather | solution.py:28
  17.4 361.8 %all-gather.19.cloned.1.call-start = ((), (), s32[]{:S(2)}) async-start(), calls=%async_computation.15 | async-start | bytes 11796480 | tf_op jit(solution)/shard_map/all_gather | solution.py:28
  18.0 747.0 %reduce-scatter.17.cloned.1.call-start = ((), (), s32[]{:S(2)}) async-start(), calls=%async_computation.11 | async-start | bytes 11796480 | tf_op jit(solution)/shard_map/reduce_scatter | solution.py:31
  29.5 0.6 copy-start.1
  30.1 104.1 %copy-start.3 = (f32[2048]{0:T(1024)}, f32[2048]{0:T(1024)S(1)}, u32[]{:S(2)}) copy-start(f32[2048]{0:T(1024)S(1)} %fusion.79) | copy-start | bytes 24580
  225.5 59.5 %copy-start.8 = (f32[2048]{0:T(1024)}, f32[2048]{0:T(1024)S(1)}, u32[]{:S(2)}) copy-start(f32[2048]{0:T(1024)S(1)} %get-tuple-element.22) | copy-start | bytes 24580
  225.5 153.7 %copy-start.5 = (f32[2048]{0:T(1024)}, f32[2048]{0:T(1024)S(1)}, u32[]{:S(2)}) copy-start(f32[2048]{0:T(1024)S(1)} %fusion.80) | copy-start | bytes 24580
  464.6 300.4 %reduce-scatter.15.cloned.1.call-start = ((), (), s32[]{:S(2)}) async-start(), calls=%async_computation.10 | async-start | bytes 11796480 | tf_op jit(solution)/shard_map/reduce_scatter | solution.py:31
  493.7 37.1 %copy-start.9 = (f32[2048]{0:T(1024)S(1)}, f32[2048]{0:T(1024)}, u32[]{:S(2)}) copy-start(f32[2048]{0:T(1024)} %copy-done.8) | copy-start | bytes 24580
  493.7 37.1 %copy-start.6 = (f32[2048]{0:T(1024)S(1)}, f32[2048]{0:T(1024)}, u32[]{:S(2)}) copy-start(f32[2048]{0:T(1024)} %copy-done.5) | copy-start | bytes 24580
  571.2 47.7 %slice-start = ((s8[5242880]{0:T(1024)(128)(4,1)}), s8[1048576]{0:T(1024)(128)(4,1)S(1)}, s32[]{:S(2)}) async-start(s8[5242880]{0:T(1024)(128)(4,1)} %bitcast.92), calls=%async_computation.19 | async-start | bytes 2097152
  571.2 193.8 %reduce-scatter.11.cloned.1.call-start = ((), (), s32[]{:S(2)}) async-start(), calls=%async_computation.8 | async-start | bytes 11796480 | tf_op jit(solution)/shard_map/reduce_scatter | solution.py:31
  571.2 47.6 %slice-start.1 = ((s8[5242880]{0:T(1024)(128)(4,1)}), s8[4194304]{0:T(1024)(128)(4,1)S(1)}, s32[]{:S(2)}) async-start(s8[5242880]{0:T(1024)(128)(4,1)} %bitcast.92), calls=%async_computation.20 | async-start | bytes 8388608
  571.3 47.6 %copy-start.4 = (f32[2048]{0:T(1024)S(1)}, f32[2048]{0:T(1024)}, u32[]{:S(2)}) copy-start(f32[2048]{0:T(1024)} %copy-done.3) | copy-start | bytes 24580
  648.4 0.7 copy-start.7
  648.5 155.2 %reduce-scatter.13.cloned.1.call-start = ((), (), s32[]{:S(2)}) async-start(), calls=%async_computation.9 | async-start | bytes 11796480 | tf_op jit(solution)/shard_map/reduce_scatter | solution.py:31
  680.0 202.4 %reduce-scatter.9.cloned.1.call-start = ((), (), s32[]{:S(2)}) async-start(), calls=%async_computation.7 | async-start | bytes 11796480 | tf_op jit(solution)/shard_map/reduce_scatter | solution.py:31
  707.9 253.0 %reduce-scatter.7.cloned.1.call-start = ((), (), s32[]{:S(2)}) async-start(), calls=%async_computation.6 | async-start | bytes 11796480 | tf_op jit(solution)/shard_map/reduce_scatter | solution.py:31
  735.8 411.5 %all-reduce.3.cloned.1.call-start = ((), (), s32[]{:S(2)}) async-start(), calls=%async_computation.18 | async-start | bytes 15728640 | tf_op jit(solution)/shard_map/psum | solution.py:31
  960.9 37.2 %copy-start.2 = (f32[2048]{0:T(1024)S(1)}, f32[2048]{0:T(1024)}, u32[]{:S(2)}) copy-start(f32[2048]{0:T(1024)} %copy-done.1) | copy-start | bytes 24580
Sparse Core Ops, SparseCore 0:
  11.0 62.0 all-gather.12
  74.9 59.1 all-gather.14
  136.0 59.1 all-gather.16
  197.0 59.1 all-gather.20
  258.5 59.2 all-gather.22
  320.0 59.1 all-gather.18
  464.7 75.1 reduce-scatter.16
  571.3 75.1 reduce-scatter.14
  650.0 75.1 reduce-scatter.10
  728.5 75.1 reduce-scatter.12
  807.2 75.1 reduce-scatter.8
  885.7 75.1 reduce-scatter.6
  964.0 183.2 all-reduce.2
where the time goes:
time: 1170 us; the launch traced here: 1160 us
  matrix products  569 us (49%)
  waiting for transfers between devices  508 us (43%)
  other arithmetic  35.9 us (3%)
  local copies, waits for them, and re-layouts  33.7 us (3%)
  between operations  14.5 us (1%)
    dot_general x6, matrix products, layer(): up = jnp.dot(a, w['w_up'], preferred_element_type=jnp.float32)  206 us
    reduce_scatter x6, waiting for transfers between devices, summed(): lax.psum_scatter(term, 's', scatter_dimension=0, tiled=True)  196 us
    dot_general x6, matrix products, layer(): gate = jnp.dot(a, w['w_gate'], preferred_element_type=jnp.float32)  193 us
    all_gather x6, waiting for transfers between devices, fetched(): lax.all_gather(w[number], 's', axis=0, tiled=True)  181 us
    dot_general x5, matrix products, matmul(): jnp.dot(a, w, preferred_element_type=jnp.float32).astype(jnp.bfloat16)  170 us
    psum x1, waiting for transfers between devices, summed(): lax.psum(lax.psum_scatter(term, 's', scatter_dimension=0, tiled=True), 'r')  129 us
    unnamed x27, local copies, waits for them, and re-layouts  24.9 us
  transfers between devices with their start and end apart: 13, of which 10 were waited for; matrix products, arithmetic and copies ran while one was open for 47% of the time, Pallas kernels for 0%

commit v1 on v0

v1 whole, which is shorter than its diff:
```python
import functools

import jax
import jax.numpy as jnp
from jax import lax
from jax.experimental import pallas as pl
from jax.experimental.pallas import tpu as pltpu
from jax.sharding import PartitionSpec as P

MESH = pl.DeviceIdType.MESH
BF, F32 = jnp.bfloat16, jnp.float32
NB = 8
LEAD = 8
TWO, THREE, FOUR = 2, 3, 4
STEPS = 11
LAST = TWO * STEPS


def nn(a, b):
    return lax.dot_general(a, b, (((1,), (0,)), ((), ())), preferred_element_type=F32)


def nt(a, b):
    return lax.dot_general(a, b, (((1,), (1,)), ((), ())), preferred_element_type=F32)


def rows_of(start, size):
    return pl.ds(start if isinstance(start, int) else pl.multiple_of(start, 16), size)


def cols_of(start, size):
    return pl.ds(start if isinstance(start, int) else pl.multiple_of(start, 128), size)


def odd(i):
    return lax.rem(i, TWO)


def copy(src, dst, sem):
    return pltpu.make_async_copy(src, dst, sem)


def done(ref, sem):
    pltpu.make_async_copy(ref, ref, sem).wait()


def both(a, b):
    return jnp.logical_and(a, b)


def either(a, b):
    return jnp.logical_or(a, b)


def vmem(*shape, dtype=BF):
    return pltpu.VMEM(shape, dtype)


def dmas(*shape):
    return pltpu.SemaphoreType.DMA(shape)


class Sizes:
    def __init__(self, T, D, F):
        self.T, self.D, self.F = T, D, F
        self.RB, self.FB, self.HB = D // NB, F // NB, D // TWO
        self.FC = self.FB
        self.UC, self.UD = self.FC // TWO, self.FB // FOUR
        self.NG, self.ND = F // self.UC, FOUR
        self.TM, self.TS = T // FOUR, T // NB
        self.PR = TWO * self.RB
        self.UNITS = TWO * (self.NG + self.ND)


class Here:
    def __init__(self):
        self.r, self.s = lax.axis_index("r"), lax.axis_index("s")
        rep, r, s = lax.axis_index("rep"), self.r, self.s
        self.c = c = odd(s)
        y, x = odd(lax.div(s, TWO)), lax.div(s, FOUR)
        self.xn, self.yn, partner = s + FOUR - NB * x, s + TWO - FOUR * y, s + 1 - TWO * c
        self.far = self.xn + self.yn - s
        self.over = self.yn + c * (self.xn - self.yn)
        self.u, self.v = x + c * (y - x), y + c * (x - y)
        n1 = self.xn + c * (self.yn - self.xn)
        n2 = self.xn + self.yn - n1
        self.to_p, self.to_x, self.to_y, self.to_z = (rep, r, partner), (rep, r, self.xn), (rep, r, self.yn), (rep, 1 - r, s)
        self.to_1, self.to_2 = (rep, r, n1), (rep, r, n2)
        self.z0, self.z1, self.c0, self.c1 = r == 0, r == 1, c == 0, c == 1

    def meet(self):
        barrier = pltpu.get_barrier_semaphore()
        for dev in (self.to_p, self.to_x, self.to_y, self.to_z):
            pl.semaphore_signal(barrier, inc=1, device_id=dev, device_id_type=MESH)
        pl.semaphore_wait(barrier, FOUR)


def remote(src, dst, ss, rs, dev):
    return pltpu.make_async_remote_copy(src, dst, ss, rs, device_id=dev, device_id_type=MESH)


def normed(h):
    wide = h.astype(F32)
    scale = lax.rsqrt(jnp.mean(wide * wide, -1, keepdims=True) + 1e-6)
    return (wide * scale).astype(BF)


def gather_of(z, me, k):
    segments = (
        (0, z.NG, "gu", 0),
        (z.NG, z.ND, "d", 0),
        (z.NG + z.ND, z.NG, "gu", 1),
        (z.UNITS - z.ND, z.ND, "d", 1),
    )

    def held(kind, l, n, d):
        if kind == "gu":
            return [G.at[l, rows_of(d * z.RB, z.RB), cols_of(n * z.UC, z.UC)] for G in (k.GG, k.GU)]
        return [k.GD.at[l, rows_of(d * z.FB + n * z.UD, z.UD), :]]

    def mine(kind, l, n):
        if kind == "gu":
            return [w.at[l, :, cols_of(n * z.UC, z.UC)] for w in (k.wg, k.wu)]
        return [k.wd.at[l, rows_of(n * z.UD, z.UD), :]]

    def got(kind, l, n, sem):
        done(k.GG.at[l, pl.ds(0, n * z.PR), pl.ds(0, z.UC)] if kind == "gu" else k.GD.at[l, pl.ds(0, n * z.UD), :], sem)

    def push(srcs, dsts, ss, rs, i, dev):
        for a, b in zip(srcs, dsts, strict=True):
            remote(a, b, ss.at[i], rs.at[i], dev).start()

    def pass_on(ref, i):
        push(ref, ref, k.gsp, k.grp, i, me.to_p)

    def stage_own(kind, l, n, i):
        own, there = mine(kind, l, n), held(kind, l, n, me.s)

        @pl.when(either(me.z0, me.c0))
        def _():
            push(own, there, k.gsx, k.grx, i, me.to_x)

        @pl.when(either(me.z0, me.c1))
        def _():
            push(own, there, k.gsy, k.gry, i, me.to_y)

        push(own, there, k.gsp, k.grp, i, me.to_p)

    def stage_1(kind, l, n, i):
        hx, hy = held(kind, l, n, me.xn), held(kind, l, n, me.yn)

        @pl.when(either(me.z0, me.c0))
        def _():
            got(kind, l, 1, k.grx.at[i])

        @pl.when(either(me.z0, me.c1))
        def _():
            got(kind, l, 1, k.gry.at[i])

        @pl.when(me.z0)
        def _():
            on = held(kind, l, n, me.over)
            push(on, on, k.gsz, k.grz, i, me.to_z)
            pass_on(hx, i)
            pass_on(hy, i)

        @pl.when(both(me.z1, me.c0))
        def _():
            push(hx, hx, k.gsy, k.gry, i, me.to_y)
            pass_on(hx, i)

        @pl.when(both(me.z1, me.c1))
        def _():
            push(hy, hy, k.gsx, k.grx, i, me.to_x)
            pass_on(hy, i)

    def stage_2(kind, l, n, i):
        @pl.when(me.z1)
        def _():
            far, over = held(kind, l, n, me.far), held(kind, l, n, me.over)

            @pl.when(me.c0)
            def _():
                got(kind, l, 1, k.gry.at[i])

            @pl.when(me.c1)
            def _():
                got(kind, l, 1, k.grx.at[i])

            push(far, far, k.gsz, k.grz, i, me.to_z)
            pass_on(far, i)
            got(kind, l, 1, k.grz.at[i])
            pass_on(over, i)

    def stage_3(kind, l, n, i):
        @pl.when(me.z0)
        def _():
            got(kind, l, 1, k.grz.at[i])
            pass_on(held(kind, l, n, me.far), i)

    def stage(fn, i, low, high):
        for start, n, kind, l in segments:
            a, b = max(start, low), min(start + n, high)
            if a < b:

                @pl.when(both(i >= a, i < b))
                def _(kind=kind, l=l, start=start):
                    fn(kind, l, i - start, i)

    def tick(t, low, high, first=0, last=z.UNITS):
        t = jnp.asarray(t, jnp.int32)
        stage(stage_own, t + LEAD, low + LEAD, high + LEAD)
        for lag, fn in enumerate((stage_1, stage_2, stage_3)):
            stage(fn, t - lag, max(first, low - lag), min(last, high - lag))

    def ready(l, kind, n):
        start = next(a for a, _, kd, ll in segments if kd == kind and ll == l)
        got(kind, l, FOUR, k.grp.at[start + n])

    def begin():
        @pl.loop(0, LEAD)
        def _(i):
            stage(stage_own, i, 0, LEAD)

    def end():
        for start, n, kind, l in segments:

            @pl.loop(0, n)
            def _(i, start=start, kind=kind, l=l):
                for sem in (k.gsx, k.gsy, k.gsz):
                    got(kind, l, 1, sem.at[start + i])
                got(kind, l, FOUR, k.gsp.at[start + i])

    return tick, ready, begin, end


def loads_of(z, me, k):
    def load_gu(l, j, WG, WU, sems):
        cols = cols_of(j * z.FC, z.FC)

        @pl.loop(0, NB)
        def _(d):
            rows = rows_of(d * z.RB, z.RB)
            for n, (W, own, G) in enumerate(((WG, k.wg, k.GG), (WU, k.wu, k.GU))):

                @pl.when(d == me.s)
                def _(n=n, W=W, own=own):
                    copy(own.at[l, :, cols], W.at[rows, :], sems.at[n]).start()

                @pl.when(d != me.s)
                def _(n=n, W=W, G=G):
                    copy(G.at[l, rows, cols], W.at[rows, :], sems.at[n]).start()

    def load_d(l, j, W, sem):
        @pl.when(j == me.s)
        def _():
            copy(k.wd.at[l], W, sem).start()

        @pl.when(j != me.s)
        def _():
            copy(k.GD.at[l, rows_of(j * z.FB, z.FB), :], W, sem).start()

    return load_gu, load_d


def forward(z, me, k):
    tick, ready, gather_begin, gather_end = gather_of(z, me, k)
    load_gu, load_d = loads_of(z, me, k)
    NS, U1 = NB, z.NG + z.ND

    def put_turned(ref, a):
        turned = a.T
        for d in range(NB):
            core, px, py = d % TWO, d // FOUR, (d // TWO) % TWO
            i = TWO * px + py if core == 0 else TWO * py + px
            ref[core * z.HB + i * z.RB : core * z.HB + (i + 1) * z.RB, :] = turned[d * z.RB : (d + 1) * z.RB, :]

    def turn(A):
        def body(xb, yb, ab, bb, si, sj, so, sp):
            def fetch(m, e):
                rows = rows_of(m * z.TS, z.TS)
                copy(k.x.at[0, rows, :], xb.at[e], si.at[e]).start()
                copy(k.dy.at[0, rows, :], yb.at[e], sj.at[e]).start()

            fetch(0, 0)

            def sent(e):
                done(ab.at[e], so.at[e])
                done(bb.at[e], sp.at[e])

            @pl.loop(0, NS)
            def _(m):
                e = odd(m)
                cols = cols_of(m * z.TS, z.TS)

                @pl.when(m + 1 < NS)
                def _():
                    fetch(m + 1, 1 - e)

                done(xb.at[e], si.at[e])
                done(yb.at[e], sj.at[e])
                a = normed(xb[e])
                A[rows_of(m * z.TS, z.TS), :] = a

                @pl.when(m >= TWO)
                def _():
                    sent(e)

                put_turned(ab.at[e], a)
                bb[e] = yb[e].T
                copy(ab.at[e], k.ATH.at[0, :, cols], so.at[e]).start()
                copy(bb.at[e], k.DYT.at[:, cols], sp.at[e]).start()

                @pl.when(e == 1)
                def _():
                    tick(lax.div(m, TWO), 0, FOUR)

            sent(0)
            sent(1)

        blocks = [vmem(TWO, z.TS, z.D)] * TWO + [vmem(TWO, z.D, z.TS)] * TWO
        pl.run_scoped(body, *blocks, *[dmas(TWO)] * FOUR)

    def gate_up(l, A, hook):
        def body(WG, WU, sb, tb, ab, ws, *so):
            kept = ((sb, k.SS), (tb, k.TT), (ab, k.ACT))

            def sent(e):
                for (b, _), sem in zip(kept, so, strict=True):
                    done(b.at[e], sem.at[e])

            def fetch(j, e):
                ready(l, "gu", TWO * j)
                ready(l, "gu", TWO * j + 1)
                load_gu(l, j, WG.at[e], WU.at[e], ws.at[e])

            fetch(0, 0)

            @pl.loop(0, NB)
            def _(j):
                slot = odd(j)
                cols = cols_of(j * z.FC, z.FC)
                done(WG.at[slot], ws.at[slot, 0])
                done(WU.at[slot], ws.at[slot, 1])

                @pl.loop(0, TWO)
                def _(m):
                    @pl.when(j + m > 0)
                    def _():
                        sent(0)
                        sent(1)

                    for e in range(TWO):
                        a = A[rows_of((TWO * m + e) * z.TM, z.TM), :]
                        gate = nn(a, WG[slot])
                        up = nn(a, WU[slot])
                        sig = lax.logistic(gate)
                        sl = gate * sig
                        sb[e] = sl
                        tb[e] = up * (sig + sl * (1.0 - sig))
                        ab[e] = (sl * up).astype(BF)
                    for e in range(TWO):
                        rows = rows_of((TWO * m + e) * z.TM, z.TM)
                        for (b, to), sem in zip(kept, so, strict=True):
                            copy(b.at[e], to.at[l, rows, cols], sem.at[e]).start()
                    hook(TWO * j + m)

                    @pl.when(both(m == 1, j + 1 < NB))
                    def _():
                        fetch(j + 1, 1 - slot)

            sent(0)
            sent(1)

        weights = [vmem(TWO, z.D, z.FC)] * TWO
        tiles = [vmem(TWO, z.TM, z.FC, dtype=F32)] * TWO + [vmem(TWO, z.TM, z.FC)]
        pl.run_scoped(body, *weights, *tiles, dmas(TWO, TWO), *[dmas(TWO)] * THREE)

    def down(A, hook):
        def body(W, ab, xb, hb, tb, ws, si, sj, so, sp):
            for n in range(z.ND):
                ready(0, "d", n)

            @pl.loop(0, NB)
            def _(d):
                load_d(0, d, W.at[rows_of(d * z.FB, z.FB), :], ws.at[0])

            def fetch(m, e):
                rows = rows_of(m * z.TS, z.TS)
                copy(k.ACT.at[0, rows, :], ab.at[e], si.at[e]).start()
                copy(k.x.at[0, rows, :], xb.at[e], sj.at[e]).start()

            fetch(0, 0)
            done(W, ws.at[0])

            def sent(e):
                done(hb.at[e], so.at[e])
                done(tb.at[e], sp.at[e])

            @pl.loop(0, NS)
            def _(m):
                e = odd(m)
                rows = rows_of(m * z.TS, z.TS)

                @pl.when(m + 1 < NS)
                def _():
                    fetch(m + 1, 1 - e)

                done(ab.at[e], si.at[e])
                done(xb.at[e], sj.at[e])
                low = nn(ab[e], W[...]).astype(BF)
                h = (xb[e].astype(F32) + low.astype(F32)).astype(BF)

                @pl.when(m >= TWO)
                def _():
                    sent(e)

                hb[e] = h
                a = normed(h)
                A[rows, :] = a
                put_turned(tb.at[e], a)
                copy(hb.at[e], k.H1.at[rows, :], so.at[e]).start()
                copy(tb.at[e], k.ATH.at[1, :, cols_of(m * z.TS, z.TS)], sp.at[e]).start()
                hook(m)

            sent(0)
            sent(1)

        tiles = [vmem(TWO, z.TS, z.F)] + [vmem(TWO, z.TS, z.D)] * TWO + [vmem(TWO, z.D, z.TS)]
        pl.run_scoped(body, vmem(z.F, z.D), *tiles, dmas(1), *[dmas(TWO)] * FOUR)

    def run(A):
        gather_begin()
        turn(A)
        gate_up(0, A, lambda n: tick(n + FOUR, FOUR, U1))
        for t in (U1, U1 + 1):
            tick(t, t, t + 1)
        t2, t3 = U1 + TWO, U1 + TWO + FOUR

        def in_down(m):
            @pl.when(odd(m) == 1)
            def _():
                tick(t2 + lax.div(m, TWO), t2, t3)

        down(A, in_down)
        gate_up(1, A, lambda n: tick(n + t3, t3, t3 + z.NG, 0, U1 + z.NG))
        for t in range(U1 + z.NG, z.UNITS + TWO):
            tick(t, t, t + 1, U1 + z.NG)
        for n in range(z.ND):
            ready(1, "d", n)
        gather_end()

    pl.run_scoped(run, vmem(z.T, z.D))


def backward(z, me, k):
    load_gu, load_d = loads_of(z, me, k)
    c, u, v = me.c, me.u, me.v
    RB, FC, HB, PR, TM = z.RB, z.FC, z.HB, z.PR, z.TM
    KINDS = range(THREE)

    def place(core, i):
        return i + core * (odd(i) * TWO + lax.div(i, TWO) - i)

    def block_of(g):
        q = lax.rem(g, STEPS)
        b = lax.div(q, THREE)
        return 1 - lax.div(g, STEPS), b, q - THREE * b + lax.div(b, THREE)

    def first_row(b):
        return jnp.minimum(THREE * b, NB - THREE)

    def has(g, n):
        _, b, t = block_of(g)
        inside = both(g >= 0, g < LAST)
        if n == 0:
            return both(inside, either(b < TWO, t > 0))
        return inside if n == 1 else both(inside, t == 0)

    def halves(slot, n):
        return remote(k.SP.at[n], k.LP.at[slot, n], k.d2ds.at[n], k.d2dr.at[slot, n], me.to_p)

    def first(slot, n):
        return remote(k.S1.at[slot, n], k.L1.at[slot, n], k.s1s.at[slot, n], k.s1r.at[slot, n], me.to_1)

    def second(slot, n):
        return remote(k.S2.at[slot, n], k.L2.at[slot, n], k.s2s.at[slot, n], k.s2r.at[slot, n], me.to_2)

    def third(slot, n):
        return remote(k.S3.at[slot, n], k.L3.at[slot, n], k.s3s.at[slot, n], k.s3r.at[slot, n], me.to_z)

    def sum_1(g):
        slot = odd(g)
        for n in KINDS:

            @pl.when(has(g - TWO, n))
            def _(n=n):
                second(slot, n).wait_send()

            @pl.when(has(g, n))
            def _(n=n):
                first(slot, n).wait_recv()
                away, home = rows_of((1 - v) * RB, RB), rows_of(v * RB, RB)
                k.S2[slot, n] = (k.K1[slot, n, away, :] + k.L1[slot, n, away, :].astype(F32)).astype(BF)
                k.K2[slot, n] = k.K1[slot, n, home, :] + k.L1[slot, n, home, :].astype(F32)
                second(slot, n).start()

        pl.semaphore_signal(k.credit, inc=1, device_id=me.to_1, device_id_type=MESH)

    def sum_2(g):
        slot = odd(g)
        for n in KINDS:

            @pl.when(has(g - TWO, n))
            def _(n=n):
                third(slot, n).wait_send()

            @pl.when(has(g, n))
            def _(n=n):
                second(slot, n).wait_recv()
                k.S3[slot, n] = (k.K2[slot, n] + k.L2[slot, n].astype(F32)).astype(BF)
                third(slot, n).start()

    def sum_3(g):
        slot = odd(g)
        l, b, t = block_of(g)
        for n in KINDS:

            @pl.when(has(g - TWO, n))
            def _(n=n):
                done(k.OUT.at[slot, n], k.osem.at[slot, n])

            @pl.when(has(g, n))
            def _(n=n):
                third(slot, n).wait_recv()
                k.OUT[slot, n] = (k.S3[slot, n].astype(F32) + k.L3[slot, n].astype(F32)).astype(BF)

                @pl.when(t == 0)
                def _():
                    copy(k.OUT.at[slot, n], k.dwdt.at[l, rows_of((first_row(b) + n) * RB, RB), :], k.osem.at[slot, n]).start()

                if n < TWO:

                    @pl.when(t > 0)
                    def _():
                        to = (k.dwg, k.dwu)[n].at[l, :, cols_of((TWO * b + t - 1) * FC, FC)]
                        copy(k.OUT.at[slot, n], to, k.osem.at[slot, n]).start()

    def sums(g):
        for lag, fn in ((FOUR, sum_3), (THREE, sum_2), (TWO, sum_1)):

            @pl.when(both(g >= lag, g < LAST + lag))
            def _(lag=lag, fn=fn):
                fn(g - lag)

    def first_sent(g):
        for n in KINDS:

            @pl.when(has(g, n))
            def _(n=n):
                first(odd(g), n).wait_send()

    def slots_free(g):
        first_sent(g - TWO)

        @pl.when(g >= TWO)
        def _():
            pl.semaphore_wait(k.credit, 1)

    def start_all(made, g):
        for n in KINDS:

            @pl.when(has(g, n))
            def _(n=n):
                made(n).start()

    def layer(it, AT, DA):
        l = 1 - it
        copy(k.ATH.at[l], AT, k.lsem.at[0]).start()

        def body(WG, WU, WD, stb, DGU, ws, si, sj, sa):
            def fetch(j, m, e):
                rows, cols = rows_of(m * TM, TM), cols_of(j * FC, FC)
                copy(k.SS.at[l, rows, cols], stb.at[0, e], si.at[e]).start()
                copy(k.TT.at[l, rows, cols], stb.at[1, e], sj.at[e]).start()

            def column(q):
                own = lax.rem(TWO * (1 - u) + q, FOUR)
                return jnp.where(q < FOUR, TWO * place(1 - c, q) + 1 - c, TWO * place(c, own) + c)

            def fetch_act(q):
                copy(k.ACT.at[l, :, cols_of(column(q) * FC, FC)], DGU.at[odd(q)], sa.at[odd(q)]).start()

            load_d(l, jnp.int32(0), WD, ws.at[TWO])
            load_gu(l, jnp.int32(0), WG, WU, ws)
            fetch(jnp.int32(0), jnp.int32(0), 0)

            @pl.loop(0, FOUR)
            def _(m):
                DA[rows_of(m * TM, TM), :] = jnp.zeros((TM, z.D), F32)

            done(AT, k.lsem.at[0])

            def product(b, q):
                @pl.when(q + 1 < NB)
                def _():
                    fetch_act(q + 1)

                done(DGU.at[odd(q)], sa.at[odd(q)])
                return nn(k.DHT[rows_of(first_row(b) * RB, THREE * RB), :], DGU[odd(q)])

            def down_step(b, g):
                slot = odd(g)

                @pl.loop(0, FOUR)
                def _(q):
                    val = product(b, q).astype(BF)
                    for n in KINDS:
                        k.SP[n, rows_of(q * RB, RB), :] = val[n * RB : (n + 1) * RB]

                start_all(lambda n: halves(slot, n), g)
                slots_free(g)
                for n in KINDS:

                    @pl.when(has(g, n))
                    def _(n=n):
                        halves(slot, n).wait_recv()

                @pl.loop(0, TWO)
                def _(e):
                    val, at = product(b, e + FOUR), rows_of((TWO * (1 - u) + e) * RB, RB)
                    for n in KINDS:
                        k.S1[slot, n, rows_of(e * RB, RB), :] = (
                            val[n * RB : (n + 1) * RB] + k.LP[slot, n, at, :].astype(F32)
                        ).astype(BF)

                start_all(lambda n: first(slot, n), g)

                @pl.loop(0, TWO)
                def _(e):
                    val, at = product(b, e + FOUR + TWO), rows_of((TWO * u + e) * RB, RB)
                    for n in KINDS:
                        k.K1[slot, n, rows_of(e * RB, RB), :] = val[n * RB : (n + 1) * RB] + k.LP[slot, n, at, :].astype(F32)

                for n in KINDS:

                    @pl.when(has(g, n))
                    def _(n=n):
                        halves(slot, n).wait_send()

            def gate_up_step(j, g):
                slot = odd(g)
                done(WD, ws.at[TWO])

                @pl.loop(0, FOUR)
                def _(m):
                    e = odd(m)
                    rows = rows_of(m * TM, TM)

                    @pl.when(m + 1 < FOUR)
                    def _():
                        fetch(j, m + 1, 1 - e)

                    @pl.when(both(m + 1 == FOUR, j + 1 < NB))
                    def _():
                        fetch(j + 1, jnp.int32(0), 1 - e)

                    done(stb.at[0, e], si.at[e])
                    done(stb.at[1, e], sj.at[e])
                    dact = nt(k.DH[rows, :], WD[...]).astype(BF).astype(F32)
                    DGU[0, rows, :] = (dact * stb[1, e]).astype(BF)
                    DGU[1, rows, :] = (dact * stb[0, e]).astype(BF)

                @pl.when(j + 1 < NB)
                def _():
                    load_d(l, j + 1, WD, ws.at[TWO])

                for n in range(TWO):
                    k.SP[n] = nn(AT[rows_of((1 - c) * HB, HB), :], DGU[n]).astype(BF)
                    halves(slot, n).start()
                slots_free(g)
                out, keep = TWO * (1 - u) * RB, TWO * u * RB
                for n in range(TWO):
                    halves(slot, n).wait_recv()
                    k.S1[slot, n] = (
                        nn(AT[rows_of(c * HB + out, PR), :], DGU[n]) + k.LP[slot, n, rows_of(out, PR), :].astype(F32)
                    ).astype(BF)
                    k.K1[slot, n] = nn(AT[rows_of(c * HB + keep, PR), :], DGU[n]) + k.LP[slot, n, rows_of(keep, PR), :].astype(F32)
                    first(slot, n).start()
                done(WG, ws.at[0])
                done(WU, ws.at[1])

                @pl.loop(0, FOUR)
                def _(m):
                    rows = rows_of(m * TM, TM)
                    DA[rows, :] += nt(DGU[0, rows, :], WG[...]) + nt(DGU[1, rows, :], WU[...])

                @pl.when(j + 1 < NB)
                def _():
                    load_gu(l, j + 1, WG, WU, ws)

                for n in range(TWO):
                    halves(slot, n).wait_send()

            @pl.loop(0, STEPS)
            def _(q):
                g = it * STEPS + q
                _, b, t = block_of(g)

                @pl.when(t == 0)
                def _():
                    fetch_act(jnp.int32(0))

                sums(g)

                @pl.when(t == 0)
                def _():
                    down_step(b, g)

                @pl.when(t > 0)
                def _():
                    gate_up_step(TWO * b + t - 1, g)

        weights = [vmem(z.D, FC)] * TWO + [vmem(z.FB, z.D)]
        tiles = [vmem(TWO, TWO, TM, FC, dtype=F32), vmem(TWO, z.T, FC)]
        pl.run_scoped(body, *weights, *tiles, dmas(THREE), *[dmas(TWO)] * THREE)
        norm_back(l, DA)

    def norm_back(l, DA):
        def body(hb, ob, si, so):
            def fetch(m, e):
                rows = rows_of(m * z.TS, z.TS)

                @pl.when(l == 1)
                def _():
                    copy(k.H1.at[rows, :], hb.at[e], si.at[e]).start()

                @pl.when(l == 0)
                def _():
                    copy(k.x.at[0, rows, :], hb.at[e], si.at[e]).start()

            fetch(jnp.int32(0), 0)

            @pl.loop(0, NB)
            def _(m):
                e = odd(m)
                rows = rows_of(m * z.TS, z.TS)

                @pl.when(m + 1 < NB)
                def _():
                    fetch(m + 1, 1 - e)

                done(hb.at[e], si.at[e])

                @pl.when(both(l == 0, m >= TWO))
                def _():
                    done(ob.at[e], so.at[e])

                wide = hb[e].astype(F32)
                da = DA[rows, :].astype(BF).astype(F32)
                scale = lax.rsqrt(jnp.mean(wide * wide, -1, keepdims=True) + 1e-6)
                along = jnp.mean(da * wide, -1, keepdims=True)
                dn = (da * scale - wide * (along * scale * scale * scale)).astype(BF)
                new = (k.DH[rows, :].astype(F32) + dn.astype(F32)).astype(BF)
                k.DH[rows, :] = new
                ob[e] = new

                @pl.when(l == 1)
                def _():
                    k.DHT[:, cols_of(m * z.TS, z.TS)] = ob[e].T

                @pl.when(l == 0)
                def _():
                    copy(ob.at[e], k.dx.at[0, rows, :], so.at[e]).start()

            @pl.when(l == 0)
            def _():
                for e in range(TWO):
                    done(ob.at[e], so.at[e])

        pl.run_scoped(body, *[vmem(TWO, z.TS, z.D)] * TWO, *[dmas(TWO)] * TWO)

    copy(k.dy.at[0], k.DH, k.lsem.at[0]).start()
    copy(k.DYT, k.DHT, k.lsem.at[1]).start()
    done(k.DH, k.lsem.at[0])
    done(k.DHT, k.lsem.at[1])

    @pl.loop(0, TWO)
    def _(it):
        pl.run_scoped(functools.partial(layer, it), vmem(z.D, z.T), vmem(z.T, z.D, dtype=F32))

    @pl.loop(LAST, LAST + FOUR)
    def _(g):
        sums(g)

    for g in (LAST - TWO, LAST - 1):
        first_sent(jnp.int32(g))
        for n in range(TWO):
            second(g % TWO, n).wait_send()
            third(g % TWO, n).wait_send()
            done(k.OUT.at[g % TWO, n], k.osem.at[g % TWO, n])
    pl.semaphore_wait(k.credit, TWO)


class Refs:
    def __init__(self, names, refs):
        for name, ref in zip(names, refs, strict=True):
            setattr(self, name, ref)


def call(name, z, fn, number, ins, outs, scratch, flops):
    names = [*ins, *outs, *scratch]

    def kernel(*refs):
        me, k = Here(), Refs(names, refs)
        me.meet()
        fn(z, me, k)

    hbm = pl.BlockSpec(memory_space=pl.ANY)
    made = pl.pallas_call(
        kernel,
        out_shape=[jax.ShapeDtypeStruct(*spec) for spec in outs.values()],
        in_specs=[hbm] * len(ins),
        out_specs=[hbm] * len(outs),
        scratch_shapes=list(scratch.values()),
        compiler_params=pltpu.CompilerParams(collective_id=number, has_side_effects=True, vmem_limit_bytes=67043328),
        cost_estimate=pl.CostEstimate(flops=flops, bytes_accessed=1 << 28, transcendentals=0),
        name=name,
    )(*ins.values())
    return dict(zip(outs, made, strict=True))


def solution(mesh):
    def step(x, dy, wg, wu, wd):
        _, T, D = x.shape
        F = wg.shape[TWO]
        z = Sizes(T, D, F)
        RB, FB, FC, L = z.RB, z.FB, z.FC, TWO
        ins = {"x": x, "dy": dy, "wg": wg, "wu": wu, "wd": wd}
        kept = {
            **{name: ((L, D, F), BF) for name in ("GG", "GU")},
            "GD": ((L, F, D), BF),
            **{name: ((L, T, F), F32) for name in ("SS", "TT")},
            "ACT": ((L, T, F), BF),
            "H1": ((T, D), BF),
            "ATH": ((L, D, T), BF),
            "DYT": ((D, T), BF),
        }
        results = {
            "dx": ((1, T, D), BF),
            **{name: ((L, RB, F), BF) for name in ("dwg", "dwu")},
            "dwdt": ((L, D, FB), BF),
        }
        gather = {name: dmas(z.UNITS) for name in ("gsx", "gsy", "gsz", "gsp", "grx", "gry", "grz", "grp")}
        item, pair = (TWO, THREE, RB, FC), (TWO, THREE, z.PR, FC)
        sums = {
            "DH": vmem(T, D),
            "DHT": vmem(D, T),
            "SP": vmem(THREE, z.HB, FC),
            "LP": vmem(TWO, THREE, z.HB, FC),
            **{name: vmem(*pair) for name in ("S1", "L1")},
            "K1": vmem(*pair, dtype=F32),
            **{name: vmem(*item) for name in ("S2", "L2", "S3", "L3", "OUT")},
            "K2": vmem(*item, dtype=F32),
            "d2ds": dmas(THREE),
            **{name: dmas(TWO, THREE) for name in ("d2dr", "s1s", "s1r", "s2s", "s2r", "s3s", "s3r", "osem")},
            "credit": pltpu.SemaphoreType.REGULAR,
            "lsem": dmas(TWO),
        }
        flops = TWO * T * D * F
        kept = call("forward", z, forward, 0, ins, kept, gather, flops * (FOUR + 1))
        made = call("backward", z, backward, 1, {**ins, **kept}, results, sums, flops * STEPS)
        return made["dx"], made["dwg"], made["dwu"], jnp.swapaxes(made["dwdt"], 1, TWO)

    states, cut = P(("rep", "r", "s"), None, None), P(None, "s", None)
    return jax.shard_map(
        step,
        mesh=mesh,
        in_specs=(states, states, cut, cut, cut),
        out_specs=(states, *[P("rep", "s", None)] * THREE),
        check_vma=False,
    )
```

time: 1170 us -> 777 us (0.66)
  Pallas kernels: 0 us -> 761 us
  matrix products: 569 us -> 0 us
  waiting for transfers between devices: 508 us -> 0 us
  other arithmetic: 35.9 us -> 0 us
  local copies, waits for them, and re-layouts: 33.7 us -> 12.7 us
  between operations: 14.5 us -> 0.65 us
    pallas_call x0 -> x2, Pallas kernels: none -> 761 us  [call(): pl.pallas_call(kernel, out_shape=[jax.ShapeDtypeStruct(*spec) for spec in...]
    dot_general x17 -> x0, matrix products: 569 us -> none  [the longest x6 206 us: layer(): up = jnp.dot(a, w['w_up'], preferred_element_type=jnp.float32)]
    reduce_scatter x6 -> x0, waiting for transfers between devices: 196 us -> none  [summed(): lax.psum_scatter(term, 's', scatter_dimension=0, tiled=True)]
    all_gather x6 -> x0, waiting for transfers between devices: 181 us -> none  [fetched(): lax.all_gather(w[number], 's', axis=0, tiled=True)]
    psum x1 -> x0, waiting for transfers between devices: 129 us -> none  [summed(): lax.psum(lax.psum_scatter(term, 's', scatter_dimension=0, tiled=True), 'r')]
    broadcast_in_dim x1 -> x0, other arithmetic: 12.3 us -> none  [step(): by_h[None]]
    add_any x1 -> x0, other arithmetic: 12.3 us -> none  [normed(): wide = h.astype(jnp.float32)]
    unnamed x27 -> x8, local copies, waits for them, and re-layouts: 24.9 us -> 12.7 us
  transfers between devices with their start and end apart: 13 -> 0, of which waited for: 10 -> 0; matrix products, arithmetic and copies ran while one was open for 47% -> 0% of each run, Pallas kernels for 0% -> 0%
where the time goes in v1:
time: 777 us; the launch traced here: 774 us
  Pallas kernels  761 us (98%)
  local copies, waits for them, and re-layouts  12.7 us (2%)
    pallas_call x2, Pallas kernels, call(): pl.pallas_call(kernel, out_shape=[jax.ShapeDtypeStruct(*spec) for spec in...  761 us

profile of v1, /device:TPU:0, one launch (start us, length us, event | category | flops | bytes accessed | tf_op | source)
XLA Modules:
  0.0 774.4 jit_solution(13507042899600414993)
XLA Ops:
  0.6 306.2 %forward.1 = (bf16[2,1280,4096]{2,1,0:T(8,128)(2,1)}, bf16[2,1280,4096]{2,1,0:T(8,128)(2,1)}, bf16[2,4096,1280]{2,1,0:T(8,128)(2,1)}, f32[2,2048,4096]{2,1,0:T(8...) custom-call(bf16[1,2048,1280]{2,1,0:T(8,128)(2,1)} %refs_0_.3, ...), custom_call_target="tpu_custom_call" | custom-call | flops 107374182400 | bytes 268435456 | tf_op jit(solution)/shard_map/forward/pallas_call | solution.py:820
  306.8 454.9 %backward.1 = (bf16[1,2048,1280]{2,1,0:T(8,128)(2,1)}, bf16[2,160,4096]{2,1,0:T(8,128)(2,1)}, bf16[2,160,4096]{2,1,0:T(8,128)(2,1)}, bf16[2,1280,512]{2,1,0:T(8,128)(2,1)}) custom-call(bf16[1,2048,1280]{2,1,0:T(8,128)(2,1)} %refs_0_.3, bf16[1,2048,1280]{2,1,0:T(8,128)(2,1)} %refs_1_.3, bf16[2,160,4096]{2,1,0:T(8,128)(2,1)} %refs_2_.3, ...), custom_call_target="tpu_custom_call" | custom-call | flops 236223201280 | bytes 268435456 | tf_op jit(solution)/shard_map/backward/pallas_call | solution.py:820
  761.7 4.4 copy.9
  766.1 0.0 copy-start.1
  766.1 0.0 copy-start
  766.1 5.3 copy.13
  771.4 0.0 copy-done.1
  771.4 1.5 copy.14
  772.9 0.0 copy-done
  772.9 1.5 copy.15
Async XLA Ops:
  766.1 5.3 copy-start.1
  766.1 6.8 copy-start

commit v2 on v1

--- a/solution.py
+++ b/solution.py
@@ -11,6 +11,7 @@
 BF, F32 = jnp.bfloat16, jnp.float32
 NB = 8
 LEAD = 8
+LAG = 2
 TWO, THREE, FOUR = 2, 3, 4
 STEPS = 11
 LAST = TWO * STEPS
@@ -210,7 +211,8 @@
     def tick(t, low, high, first=0, last=z.UNITS):
         t = jnp.asarray(t, jnp.int32)
         stage(stage_own, t + LEAD, low + LEAD, high + LEAD)
-        for lag, fn in enumerate((stage_1, stage_2, stage_3)):
+        for n, fn in enumerate((stage_1, stage_2, stage_3)):
+            lag = LAG * n
             stage(fn, t - lag, max(first, low - lag), min(last, high - lag))
 
     def ready(l, kind, n):
@@ -276,7 +278,7 @@
             ref[core * z.HB + i * z.RB : core * z.HB + (i + 1) * z.RB, :] = turned[d * z.RB : (d + 1) * z.RB, :]
 
     def turn(A):
-        def body(xb, yb, ab, bb, si, sj, so, sp):
+        def body(xb, yb, ab, si, sj, so):
             def fetch(m, e):
                 rows = rows_of(m * z.TS, z.TS)
                 copy(k.x.at[0, rows, :], xb.at[e], si.at[e]).start()
@@ -286,7 +288,6 @@
 
             def sent(e):
                 done(ab.at[e], so.at[e])
-                done(bb.at[e], sp.at[e])
 
             @pl.loop(0, NS)
             def _(m):
@@ -307,9 +308,8 @@
                     sent(e)
 
                 put_turned(ab.at[e], a)
-                bb[e] = yb[e].T
                 copy(ab.at[e], k.ATH.at[0, :, cols], so.at[e]).start()
-                copy(bb.at[e], k.DYT.at[:, cols], sp.at[e]).start()
+                k.DHT[:, cols] = yb[e].T
 
                 @pl.when(e == 1)
                 def _():
@@ -318,8 +318,8 @@
             sent(0)
             sent(1)
 
-        blocks = [vmem(TWO, z.TS, z.D)] * TWO + [vmem(TWO, z.D, z.TS)] * TWO
-        pl.run_scoped(body, *blocks, *[dmas(TWO)] * FOUR)
+        blocks = [vmem(TWO, z.TS, z.D)] * TWO + [vmem(TWO, z.D, z.TS)]
+        pl.run_scoped(body, *blocks, *[dmas(TWO)] * THREE)
 
     def gate_up(l, A, hook):
         def body(WG, WU, sb, tb, ab, ws, *so):
@@ -431,11 +431,14 @@
 
     def run(A):
         gather_begin()
+        copy(k.dy.at[0], k.DH, k.lsem.at[0]).start()
         turn(A)
-        gate_up(0, A, lambda n: tick(n + FOUR, FOUR, U1))
-        for t in (U1, U1 + 1):
+        t1, t2, t3 = TWO * LAG + TWO, U1 + TWO * LAG, U1 + TWO * LAG + FOUR
+        for t in range(FOUR, t1):
             tick(t, t, t + 1)
-        t2, t3 = U1 + TWO, U1 + TWO + FOUR
+        gate_up(0, A, lambda n: tick(n + t1, t1, t1 + z.NG))
+        for t in range(t1 + z.NG, t2):
+            tick(t, t, t + 1)
 
         def in_down(m):
             @pl.when(odd(m) == 1)
@@ -444,19 +447,23 @@
 
         down(A, in_down)
         gate_up(1, A, lambda n: tick(n + t3, t3, t3 + z.NG, 0, U1 + z.NG))
-        for t in range(U1 + z.NG, z.UNITS + TWO):
-            tick(t, t, t + 1, U1 + z.NG)
+
+    def late(n):
+        tick(n + U1 + z.NG, U1 + z.NG, U1 + z.NG + NB, U1 + z.NG)
+
+    def all_there():
         for n in range(z.ND):
             ready(1, "d", n)
-        gather_end()
 
     pl.run_scoped(run, vmem(z.T, z.D))
-
-
-def backward(z, me, k):
+    return late, all_there, gather_end
+
+
+def backward(z, me, k, late, all_there):
     load_gu, load_d = loads_of(z, me, k)
     c, u, v = me.c, me.u, me.v
     RB, FC, HB, PR, TM = z.RB, z.FC, z.HB, z.PR, z.TM
+    DR = THREE * RB
     KINDS = range(THREE)
 
     def place(core, i):
@@ -478,7 +485,13 @@
         return inside if n == 1 else both(inside, t == 0)
 
     def halves(slot, n):
-        return remote(k.SP.at[n], k.LP.at[slot, n], k.d2ds.at[n], k.d2dr.at[slot, n], me.to_p)
+        rows = pl.ds(n * HB, HB)
+        return remote(k.SP.at[rows, :], k.LP.at[slot, rows, :], k.d2ds.at[n], k.d2dr.at[slot, n], me.to_p)
+
+    def block(slot, e):
+        return remote(
+            k.SP.at[rows_of(odd(e) * DR, DR), :], k.LP.at[slot, rows_of(e * DR, DR), :], k.b2ds.at[odd(e)], k.b2dr.at[slot, e], me.to_p
+        )
 
     def first(slot, n):
         return remote(k.S1.at[slot, n], k.L1.at[slot, n], k.s1s.at[slot, n], k.s1r.at[slot, n], me.to_1)
@@ -513,7 +526,7 @@
 
             @pl.when(has(g - TWO, n))
             def _(n=n):
-                third(slot, n).wait_send()
+                done(k.S3.at[slot, n], k.osem.at[slot, n])
 
             @pl.when(has(g, n))
             def _(n=n):
@@ -526,25 +539,21 @@
         l, b, t = block_of(g)
         for n in KINDS:
 
-            @pl.when(has(g - TWO, n))
-            def _(n=n):
-                done(k.OUT.at[slot, n], k.osem.at[slot, n])
-
             @pl.when(has(g, n))
             def _(n=n):
-                third(slot, n).wait_recv()
-                k.OUT[slot, n] = (k.S3[slot, n].astype(F32) + k.L3[slot, n].astype(F32)).astype(BF)
+                third(slot, n).wait()
+                k.S3[slot, n] = (k.S3[slot, n].astype(F32) + k.L3[slot, n].astype(F32)).astype(BF)
 
                 @pl.when(t == 0)
                 def _():
-                    copy(k.OUT.at[slot, n], k.dwdt.at[l, rows_of((first_row(b) + n) * RB, RB), :], k.osem.at[slot, n]).start()
+                    copy(k.S3.at[slot, n], k.dwdt.at[l, rows_of((first_row(b) + n) * RB, RB), :], k.osem.at[slot, n]).start()
 
                 if n < TWO:
 
                     @pl.when(t > 0)
                     def _():
                         to = (k.dwg, k.dwu)[n].at[l, :, cols_of((TWO * b + t - 1) * FC, FC)]
-                        copy(k.OUT.at[slot, n], to, k.osem.at[slot, n]).start()
+                        copy(k.S3.at[slot, n], to, k.osem.at[slot, n]).start()
 
     def sums(g):
         for lag, fn in ((FOUR, sum_3), (THREE, sum_2), (TWO, sum_1)):
@@ -567,33 +576,29 @@
         def _():
             pl.semaphore_wait(k.credit, 1)
 
-    def start_all(made, g):
-        for n in KINDS:
-
-            @pl.when(has(g, n))
-            def _(n=n):
-                made(n).start()
-
     def layer(it, AT, DA):
         l = 1 - it
         copy(k.ATH.at[l], AT, k.lsem.at[0]).start()
 
         def body(WG, WU, WD, stb, DGU, ws, si, sj, sa):
-            def fetch(j, m, e):
-                rows, cols = rows_of(m * TM, TM), cols_of(j * FC, FC)
+            def fetch(i):
+                rows, cols = rows_of(lax.rem(i, FOUR) * TM, TM), cols_of(lax.div(i, FOUR) * FC, FC)
+                e = lax.rem(i, THREE)
                 copy(k.SS.at[l, rows, cols], stb.at[0, e], si.at[e]).start()
                 copy(k.TT.at[l, rows, cols], stb.at[1, e], sj.at[e]).start()
 
             def column(q):
-                own = lax.rem(TWO * (1 - u) + q, FOUR)
-                return jnp.where(q < FOUR, TWO * place(1 - c, q) + 1 - c, TWO * place(c, own) + c)
+                theirs, own = lax.rem(TWO * (1 - v) + q, FOUR), lax.rem(TWO * (1 - u) + q, FOUR)
+                return jnp.where(q < FOUR, TWO * place(1 - c, theirs) + 1 - c, TWO * place(c, own) + c)
 
             def fetch_act(q):
-                copy(k.ACT.at[l, :, cols_of(column(q) * FC, FC)], DGU.at[odd(q)], sa.at[odd(q)]).start()
-
-            load_d(l, jnp.int32(0), WD, ws.at[TWO])
+                e = lax.rem(q + TWO, THREE)
+                copy(k.ACT.at[l, :, cols_of(column(q) * FC, FC)], DGU.at[e], sa.at[e]).start()
+
             load_gu(l, jnp.int32(0), WG, WU, ws)
-            fetch(jnp.int32(0), jnp.int32(0), 0)
+            fetch_act(jnp.int32(0))
+            fetch(jnp.int32(0))
+            fetch(jnp.int32(1))
 
             @pl.loop(0, FOUR)
             def _(m):
@@ -602,51 +607,67 @@
             done(AT, k.lsem.at[0])
 
             def product(b, q):
-                @pl.when(q + 1 < NB)
-                def _():
-                    fetch_act(q + 1)
-
-                done(DGU.at[odd(q)], sa.at[odd(q)])
-                return nn(k.DHT[rows_of(first_row(b) * RB, THREE * RB), :], DGU[odd(q)])
+                e = lax.rem(q + TWO, THREE)
+
+                @pl.when(both(q > 0, q + TWO < NB))
+                def _():
+                    fetch_act(q + TWO)
+
+                @pl.when(both(it == 0, b == 0))
+                def _():
+                    late(q)
+
+                done(DGU.at[e], sa.at[e])
+                return nn(k.DHT[rows_of(first_row(b) * RB, DR), :], DGU[e])
 
             def down_step(b, g):
                 slot = odd(g)
+                fetch_act(jnp.int32(1))
+                fetch_act(jnp.int32(TWO))
 
                 @pl.loop(0, FOUR)
-                def _(q):
-                    val = product(b, q).astype(BF)
+                def _(e):
+                    val = product(b, e).astype(BF)
+
+                    @pl.when(e >= TWO)
+                    def _():
+                        block(slot, e - TWO).wait_send()
+
+                    k.SP[rows_of(odd(e) * DR, DR), :] = val
+                    block(slot, e).start()
+
+                slots_free(g)
+
+                @pl.loop(0, TWO)
+                def _(e):
+                    block(slot, e).wait_recv()
+                    val = (product(b, e + FOUR) + k.LP[slot, rows_of(e * DR, DR), :].astype(F32)).astype(BF)
                     for n in KINDS:
-                        k.SP[n, rows_of(q * RB, RB), :] = val[n * RB : (n + 1) * RB]
-
-                start_all(lambda n: halves(slot, n), g)
-                slots_free(g)
+                        k.S1[slot, n, rows_of(e * RB, RB), :] = val[n * RB : (n + 1) * RB]
+
                 for n in KINDS:
 
                     @pl.when(has(g, n))
                     def _(n=n):
-                        halves(slot, n).wait_recv()
+                        first(slot, n).start()
 
                 @pl.loop(0, TWO)
                 def _(e):
-                    val, at = product(b, e + FOUR), rows_of((TWO * (1 - u) + e) * RB, RB)
+                    block(slot, e + TWO).wait_recv()
+                    val = product(b, e + FOUR + TWO) + k.LP[slot, rows_of((e + TWO) * DR, DR), :].astype(F32)
                     for n in KINDS:
-                        k.S1[slot, n, rows_of(e * RB, RB), :] = (
-                            val[n * RB : (n + 1) * RB] + k.LP[slot, n, at, :].astype(F32)
-                        ).astype(BF)
-
-                start_all(lambda n: first(slot, n), g)
-
-                @pl.loop(0, TWO)
-                def _(e):
-                    val, at = product(b, e + FOUR + TWO), rows_of((TWO * u + e) * RB, RB)
-                    for n in KINDS:
-                        k.K1[slot, n, rows_of(e * RB, RB), :] = val[n * RB : (n + 1) * RB] + k.LP[slot, n, at, :].astype(F32)
-
-                for n in KINDS:
-
-                    @pl.when(has(g, n))
-                    def _(n=n):
-                        halves(slot, n).wait_send()
+                        k.K1[slot, n, rows_of(e * RB, RB), :] = val[n * RB : (n + 1) * RB]
+
+                for e in range(TWO):
+                    block(slot, e).wait_send()
+
+                @pl.when(b == 0)
+                def _():
+                    @pl.when(it == 0)
+                    def _():
+                        all_there()
+
+                    load_d(l, jnp.int32(0), WD, ws.at[TWO])
 
             def gate_up_step(j, g):
                 slot = odd(g)
@@ -654,16 +675,13 @@
 
                 @pl.loop(0, FOUR)
                 def _(m):
-                    e = odd(m)
+                    i = j * FOUR + m
+                    e = lax.rem(i, THREE)
                     rows = rows_of(m * TM, TM)
 
-                    @pl.when(m + 1 < FOUR)
+                    @pl.when(i + TWO < FOUR * NB)
                     def _():
-                        fetch(j, m + 1, 1 - e)
-
-                    @pl.when(both(m + 1 == FOUR, j + 1 < NB))
-                    def _():
-                        fetch(j + 1, jnp.int32(0), 1 - e)
+                        fetch(i + TWO)
 
                     done(stb.at[0, e], si.at[e])
                     done(stb.at[1, e], sj.at[e])
@@ -676,16 +694,16 @@
                     load_d(l, j + 1, WD, ws.at[TWO])
 
                 for n in range(TWO):
-                    k.SP[n] = nn(AT[rows_of((1 - c) * HB, HB), :], DGU[n]).astype(BF)
+                    k.SP[n * HB : (n + 1) * HB, :] = nn(AT[rows_of((1 - c) * HB, HB), :], DGU[n]).astype(BF)
                     halves(slot, n).start()
                 slots_free(g)
                 out, keep = TWO * (1 - u) * RB, TWO * u * RB
                 for n in range(TWO):
                     halves(slot, n).wait_recv()
                     k.S1[slot, n] = (
-                        nn(AT[rows_of(c * HB + out, PR), :], DGU[n]) + k.LP[slot, n, rows_of(out, PR), :].astype(F32)
+                        nn(AT[rows_of(c * HB + out, PR), :], DGU[n]) + k.LP[slot, rows_of(n * HB + out, PR), :].astype(F32)
                     ).astype(BF)
-                    k.K1[slot, n] = nn(AT[rows_of(c * HB + keep, PR), :], DGU[n]) + k.LP[slot, n, rows_of(keep, PR), :].astype(F32)
+                    k.K1[slot, n] = nn(AT[rows_of(c * HB + keep, PR), :], DGU[n]) + k.LP[slot, rows_of(n * HB + keep, PR), :].astype(F32)
                     first(slot, n).start()
                 done(WG, ws.at[0])
                 done(WU, ws.at[1])
@@ -699,6 +717,10 @@
                 def _():
                     load_gu(l, j + 1, WG, WU, ws)
 
+                @pl.when(both(lax.rem(j, TWO) == 1, j + TWO + 1 < NB))
+                def _():
+                    fetch_act(jnp.int32(0))
+
                 for n in range(TWO):
                     halves(slot, n).wait_send()
 
@@ -706,15 +728,10 @@
             def _(q):
                 g = it * STEPS + q
                 _, b, t = block_of(g)
+                sums(g)
 
                 @pl.when(t == 0)
                 def _():
-                    fetch_act(jnp.int32(0))
-
-                sums(g)
-
-                @pl.when(t == 0)
-                def _():
                     down_step(b, g)
 
                 @pl.when(t > 0)
@@ -722,8 +739,8 @@
                     gate_up_step(TWO * b + t - 1, g)
 
         weights = [vmem(z.D, FC)] * TWO + [vmem(z.FB, z.D)]
-        tiles = [vmem(TWO, TWO, TM, FC, dtype=F32), vmem(TWO, z.T, FC)]
-        pl.run_scoped(body, *weights, *tiles, dmas(THREE), *[dmas(TWO)] * THREE)
+        tiles = [vmem(TWO, THREE, TM, FC, dtype=F32), vmem(THREE, z.T, FC)]
+        pl.run_scoped(body, *weights, *tiles, *[dmas(THREE)] * FOUR)
         norm_back(l, DA)
 
     def norm_back(l, DA):
@@ -780,10 +797,7 @@
 
         pl.run_scoped(body, *[vmem(TWO, z.TS, z.D)] * TWO, *[dmas(TWO)] * TWO)
 
-    copy(k.dy.at[0], k.DH, k.lsem.at[0]).start()
-    copy(k.DYT, k.DHT, k.lsem.at[1]).start()
     done(k.DH, k.lsem.at[0])
-    done(k.DHT, k.lsem.at[1])
 
     @pl.loop(0, TWO)
     def _(it):
@@ -797,8 +811,7 @@
         first_sent(jnp.int32(g))
         for n in range(TWO):
             second(g % TWO, n).wait_send()
-            third(g % TWO, n).wait_send()
-            done(k.OUT.at[g % TWO, n], k.osem.at[g % TWO, n])
+            done(k.S3.at[g % TWO, n], k.osem.at[g % TWO, n])
     pl.semaphore_wait(k.credit, TWO)
 
 
@@ -844,7 +857,6 @@
             "ACT": ((L, T, F), BF),
             "H1": ((T, D), BF),
             "ATH": ((L, D, T), BF),
-            "DYT": ((D, T), BF),
         }
         results = {
             "dx": ((1, T, D), BF),
@@ -856,20 +868,28 @@
         sums = {
             "DH": vmem(T, D),
             "DHT": vmem(D, T),
-            "SP": vmem(THREE, z.HB, FC),
-            "LP": vmem(TWO, THREE, z.HB, FC),
+            "SP": vmem(TWO * z.HB, FC),
+            "LP": vmem(TWO, THREE * z.HB, FC),
             **{name: vmem(*pair) for name in ("S1", "L1")},
             "K1": vmem(*pair, dtype=F32),
-            **{name: vmem(*item) for name in ("S2", "L2", "S3", "L3", "OUT")},
+            **{name: vmem(*item) for name in ("S2", "L2", "S3", "L3")},
             "K2": vmem(*item, dtype=F32),
-            "d2ds": dmas(THREE),
-            **{name: dmas(TWO, THREE) for name in ("d2dr", "s1s", "s1r", "s2s", "s2r", "s3s", "s3r", "osem")},
+            "d2ds": dmas(TWO),
+            "d2dr": dmas(TWO, TWO),
+            "b2ds": dmas(TWO),
+            "b2dr": dmas(TWO, FOUR),
+            **{name: dmas(TWO, THREE) for name in ("s1s", "s1r", "s2s", "s2r", "s3s", "s3r", "osem")},
             "credit": pltpu.SemaphoreType.REGULAR,
-            "lsem": dmas(TWO),
+            "lsem": dmas(1),
         }
         flops = TWO * T * D * F
-        kept = call("forward", z, forward, 0, ins, kept, gather, flops * (FOUR + 1))
-        made = call("backward", z, backward, 1, {**ins, **kept}, results, sums, flops * STEPS)
+
+        def whole(z, me, k):
+            late, all_there, gather_end = forward(z, me, k)
+            backward(z, me, k, late, all_there)
+            gather_end()
+
+        made = call("whole", z, whole, 0, ins, {**results, **kept}, {**gather, **sums}, flops * (STEPS + FOUR + TWO))
         return made["dx"], made["dwg"], made["dwu"], jnp.swapaxes(made["dwdt"], 1, TWO)
 
     states, cut = P(("rep", "r", "s"), None, None), P(None, "s", None)

time: 777 us -> 706 us (0.909)
  Pallas kernels: 761 us -> 691 us
    pallas_call x2 -> x1, Pallas kernels: 761 us -> 691 us  [call(): pl.pallas_call(kernel, out_shape=[jax.ShapeDtypeStruct(*spec) for spec in...]
where the time goes in v2:
time: 706 us; the launch traced here: 705 us
  Pallas kernels  691 us (98%)
  local copies, waits for them, and re-layouts  12.7 us (2%)
    pallas_call x1, Pallas kernels, call(): pl.pallas_call(kernel, out_shape=[jax.ShapeDtypeStruct(*spec) for spec in...  691 us

profile of v2, /device:TPU:0, one launch (start us, length us, event | category | flops | bytes accessed | tf_op | source)
XLA Modules:
  0.0 704.6 jit_solution(1964303940747042553)
XLA Ops:
  0.6 691.2 %whole.1 = (bf16[1,2048,1280]{2,1,0:T(8,128)(2,1)}, bf16[2,160,4096]{2,1,0:T(8,128)(2,1)}, bf16[2,160,4096]{2,1,0:T(8,128)(2,1)}, bf16[2,1280,512]{2,1,0:T(8,128...) custom-call(bf16[1,2048,1280]{2,1,0:T(8,128)(2,1)} %refs_0_.1, ...), custom_call_target="tpu_custom_call" | custom-call | flops 365072220160 | bytes 268435456 | tf_op jit(solution)/shard_map/whole/pallas_call | solution.py:833
  691.8 4.4 copy.9
  696.2 0.0 copy-start.1
  696.2 0.0 copy-start
  696.2 5.3 copy.13
  701.6 0.0 copy-done.1
  701.6 1.5 copy.14
  703.1 0.0 copy-done
  703.1 1.5 copy.15
Async XLA Ops:
  696.2 5.3 copy-start.1
  696.2 6.8 copy-start
